TPU v7x, 256 devices: a whole 4x4x8 slice. The times are simulated.
256 devices in a mesh: site: 32 (over z, y), ka: 8 (over x, core).
Axes of the slice: x: 4, y: 4, z: 8, core: 2. Of those that a mesh axis runs over, the one named last changes fastest.
Arguments:
- positions: float32 [3, 512], P(None, 'site'), may hold values from 0 to 1
- site_class: int32 [512], P('site'), may hold values from 0 to 3
- class_charge: float32 [4], replicated, may hold values from -2 to 2
- miller: int32 [3, 1048576], P(None, 'ka'), may hold values from -80 to 80, as said below
Outputs:
- forces: float32 [3, 512], P(None, ('site', 'ka'))
- energy: float32 [], replicated
Inputs may be any that keep to these rules, and one draw needn't show every extreme that they name: `miller`: the k-vectors are all distinct, and none has all three indices zero.
All inputs are finite; a program needn't handle non-finite values.
Results may differ from a plain program's by a relative error of at most 0.0003.
Values sent between devices are 32-bit elements; how exact they have to be, the bound alone decides.
A program may use at most 64 MiB of HBM per device.

v0:
```python
import math

import jax
import jax.numpy as jnp
from jax import lax
from jax.sharding import Mesh
from jax.sharding import PartitionSpec as P

KBLOCK = 4096
MMAX = 80
NCLS = 4
SITE = ("site_0", "site_1")
KA = ("ka_0", "ka_1")
SITE_KA = ("site_0", "site_1", "ka_0", "ka_1")


def in_order(blocks, dim):
    blocks = jnp.moveaxis(blocks, 0, dim)
    dims = blocks.shape
    return blocks.reshape(*dims[:dim], dims[dim] * dims[dim + 1], *dims[dim + 2 :])


def from_everyone(array, axis):
    peers = lax.axis_size(axis)
    return lax.all_to_all(
        jnp.broadcast_to(array[None], (peers, *array.shape)), axis, 0, 0, tiled=True
    )


def collect(array, axis, dim):
    return in_order(from_everyone(array, axis), dim)


def split_up(array, dim, peers):
    before, after = (array.shape[:dim], array.shape[dim + 1 :])
    return jnp.moveaxis(array.reshape(*before, peers, -1, *after), dim, 0)


def summed_on_arrival(array, axis, dim):
    peers = lax.axis_size(axis)
    blocks = lax.all_to_all(split_up(array, dim, peers), axis, 0, 0, tiled=True)
    return jnp.sum(blocks, axis=0)


def summed_rows(array, axes, dim):
    far, near = axes
    blocks = split_up(array, dim, lax.axis_size(far))
    nearer = summed_on_arrival(blocks, near, dim + 1)
    arrived = lax.all_to_all(nearer, far, split_axis=0, concat_axis=0, tiled=True)
    return arrived.sum(axis=0)


def over_copies(array, axis):
    everything = from_everyone(array, axis)
    return jnp.sum(everything, axis=0)


def one_axis_at_a_time(array, axes):
    far, near = axes
    return over_copies(over_copies(array, near), far)


def charges_of(site_class, class_charge):
    onehot = (site_class[None, :] == jnp.arange(NCLS, dtype=jnp.int32)[:, None]).astype(jnp.float32)
    return jnp.dot(class_charge, onehot, precision=lax.Precision.HIGHEST)


def kernel_weights(mfloat):
    square = jnp.sum(mfloat * mfloat, axis=0)
    limit = float(MMAX * MMAX)
    return limit * jnp.exp(-square / limit) / square


def phases(mblock, positions):
    angles = (
        2.0
        * math.pi
        * (
            mblock[0][:, None] * positions[0][None, :]
            + mblock[1][:, None] * positions[1][None, :]
            + mblock[2][:, None] * positions[2][None, :]
        )
    )
    return (jnp.cos(angles), jnp.sin(angles))


def force_terms(mblock, real_part, imag_part, wblock, cosine, sine):
    grad_sine = mblock * (wblock * real_part)[None, :]
    grad_cosine = mblock * (wblock * imag_part)[None, :]
    return jnp.dot(grad_sine, sine, precision=lax.Precision.HIGHEST) - jnp.dot(
        grad_cosine, cosine, precision=lax.Precision.HIGHEST
    )


def local(positions, site_class, class_charge, miller):
    local_sites = positions.shape[1]
    local_kvecs = miller.shape[1]
    nsites_all = local_sites * lax.axis_size(SITE)
    kvecs_all = local_kvecs * lax.axis_size(KA)
    charge = charges_of(site_class, class_charge)
    mfloat = miller.astype(jnp.float32)
    scale = 1.0 / math.sqrt(nsites_all)
    force_scale = 4.0 * math.pi / math.sqrt(nsites_all * kvecs_all)
    packed = jnp.concatenate([positions, charge[None, :]], axis=0)
    gathered = collect(packed, SITE, 1)
    all_positions = gathered[:3]
    all_charge = gathered[3]
    sub_count = local_kvecs // lax.axis_size(SITE)
    block_rows = KBLOCK // lax.axis_size(SITE)
    my_kvecs = lax.dynamic_slice_in_dim(mfloat, lax.axis_index(SITE) * sub_count, sub_count, 1)
    my_weights = kernel_weights(my_kvecs)
    nblocks = sub_count // block_rows
    my_blocks = my_kvecs.reshape(3, nblocks, block_rows).transpose(1, 0, 2)
    my_wblocks = my_weights.reshape(nblocks, block_rows)

    def gather_step(total, items):
        mblock, wblock = items
        cosine, sine = phases(mblock, all_positions)
        real_part = jnp.dot(cosine, all_charge, precision=lax.Precision.HIGHEST) * scale
        imag_part = jnp.dot(sine, all_charge, precision=lax.Precision.HIGHEST) * scale
        total = total + force_terms(mblock, real_part, imag_part, wblock, cosine, sine)
        return (total, jnp.sum(wblock * (real_part * real_part + imag_part * imag_part)))

    total, energy_terms = lax.scan(
        gather_step, jnp.zeros((3, nsites_all), jnp.float32), (my_blocks, my_wblocks)
    )
    forces_local = force_scale * all_charge[None, :] * total
    forces = summed_rows(forces_local, (("site_0", "site_1"), ("ka_0", "ka_1")), 1)
    energy_sum = one_axis_at_a_time(jnp.sum(energy_terms), (("site_0", "site_1"), ("ka_0", "ka_1")))
    return (forces, energy_sum / kvecs_all)


def solution(mesh):
    torus = Mesh(mesh.devices.reshape(8, 4, 4, 2), ("site_0", "site_1", "ka_0", "ka_1"))
    placed = (P(None, SITE), P(SITE), P(), P(None, KA))
    return jax.shard_map(
        local, mesh=torus, in_specs=placed, out_specs=(P(None, SITE_KA), P()), check_vma=False
    )
```

profile of v0, /device:TPU:1, one launch (start us, length us, event | category | flops | bytes accessed | tf_op | source)
XLA Modules:
  0.0 282.6 jit_solution(786149963495031824)
XLA Ops:
  3.4 12.0 %all-to-all-start = ((f32[32,4,16]{2,1,0:T(4,128)}), f32[32,4,16]{2,1,0:T(4,128)S(1)}, u32[]{:S(2)}, u32[]{:S(2)}) async-start(f32[32,4,16]{2,1,0:T(4,128)} %broadcast_in_dim.19), calls=%async_computation | async-start | bytes 131072 | tf_op jit(solution)/shard_map/all_to_all | solution.py:25
  17.2 7.0 %all-to-all-done = f32[32,4,16]{2,1,0:T(4,128)S(1)} async-done(((f32[32,4,16]{2,1,0:T(4,128)}), f32[32,4,16]{2,1,0:T(4,128)S(1)}, u32[]{:S(2)}, u32[]{:S(2)}) %all-to-all-start) | async-done | bytes 8224 | tf_op jit(solution)/shard_map/all_to_all | solution.py:25
  24.5 208.9 %while.13 = (s32[]{:T(128)}, f32[3,512]{1,0:T(4,128)S(1)}, f32[32]{0:T(128)S(1)}, f32[32,3,128]{2,1,0:T(4,128)S(1)}, f32[32,128]{1,0:T(8,128)S(1)}, /*index=5*/f...) while((s32[]{:T(128)}, f32[3,512]{1,0:T(4,128)S(1)}, f32[32]{0:T(128)S(1)}, ...), condition=%wide.region_3.4_spmd.clone, body=%wide.region_1.3_spmd.clone.sunk | while | flops 7870850 | bytes 84615 | solution.py:124
  25.8 2.0 fusion.72
  32.3 2.0 fusion.72
  38.9 2.0 fusion.72
  45.4 2.0 fusion.72
  51.9 2.0 fusion.72
  58.4 2.0 fusion.72
  65.0 2.0 fusion.72
  71.5 2.0 fusion.72
  78.0 2.0 fusion.72
  130.3 2.0 fusion.72
  136.8 2.0 fusion.72
  143.3 2.0 fusion.72
  149.8 2.0 fusion.72
  235.2 6.4 %all-to-all-start.3 = ((f32[8,1,1]{2,1,0:T(1,128)}), f32[8,1,1]{2,1,0:T(1,128)S(1)}, u32[]{:S(2)}, u32[]{:S(2)}) async-start(f32[8,1,1]{2,1,0:T(1,128)} %broadcast_in_dim.22), calls=%async_computation.3 | async-start | bytes 8192 | tf_op jit(solution)/shard_map/all_to_all | solution.py:25
  242.5 3.7 %all-to-all-done.3 = f32[8,1,1]{2,1,0:T(1,128)S(1)} async-done(((f32[8,1,1]{2,1,0:T(1,128)}), f32[8,1,1]{2,1,0:T(1,128)S(1)}, u32[]{:S(2)}, u32[]{:S(2)}) %all-to-all-start.3) | async-done | bytes 64 | tf_op jit(solution)/shard_map/all_to_all | solution.py:25
  246.2 3.9 %all-to-all-start.1 = ((f32[8,1,192]{2,1,0:T(1,128)}), f32[8,1,192]{2,1,0:T(1,128)S(1)}, u32[]{:S(2)}, u32[]{:S(2)}) async-start(f32[8,1,192]{2,1,0:T(1,128)} %reshape.61), calls=%async_computation.1 | async-start | bytes 16384 | tf_op jit(solution)/shard_map/all_to_all | solution.py:41
  250.8 4.0 %all-to-all-done.1 = f32[8,1,192]{2,1,0:T(1,128)S(1)} async-done(((f32[8,1,192]{2,1,0:T(1,128)}), f32[8,1,192]{2,1,0:T(1,128)S(1)}, u32[]{:S(2)}, u32[]{:S(2)}) %all-to-all-start.1) | async-done | bytes 6176 | tf_op jit(solution)/shard_map/all_to_all | solution.py:41
  256.1 3.8 %all-to-all-start.4 = ((f32[32,1,1]{2,1,0:T(1,128)}), f32[32,1,1]{2,1,0:T(1,128)S(1)}, u32[]{:S(2)}, u32[]{:S(2)}) async-start(f32[32,1,1]{2,1,0:T(1,128)} %broadcast_in_dim.40), calls=%async_computation.4 | async-start | bytes 32768 | tf_op jit(solution)/shard_map/all_to_all | solution.py:25
  261.9 6.5 %all-to-all-done.4 = f32[32,1,1]{2,1,0:T(1,128)S(1)} async-done(((f32[32,1,1]{2,1,0:T(1,128)}), f32[32,1,1]{2,1,0:T(1,128)S(1)}, u32[]{:S(2)}, u32[]{:S(2)}) %all-to-all-start.4) | async-done | bytes 160 | tf_op jit(solution)/shard_map/all_to_all | solution.py:25
  268.3 3.9 %all-to-all-start.2 = ((f32[32,3,2]{1,2,0:T(2,128)}), f32[32,3,2]{1,2,0:T(2,128)S(1)}, u32[]{:S(2)}, u32[]{:S(2)}) async-start(f32[32,3,2]{1,2,0:T(2,128)} %copy.21), calls=%async_computation.2 | async-start | bytes 65536 | tf_op jit(solution)/shard_map/all_to_all | solution.py:49
  273.5 7.3 %all-to-all-done.2 = f32[32,3,2]{1,2,0:T(2,128)S(1)} async-done(((f32[32,3,2]{1,2,0:T(2,128)}), f32[32,3,2]{1,2,0:T(2,128)S(1)}, u32[]{:S(2)}, u32[]{:S(2)}) %all-to-all-start.2) | async-done | bytes 800 | tf_op jit(solution)/shard_map/all_to_all | solution.py:49
  (274 shorter events, 194.3 us)
Async XLA Ops:
  0.6 0.7 copy-start
  3.4 20.8 %all-to-all-start = ((f32[32,4,16]{2,1,0:T(4,128)}), f32[32,4,16]{2,1,0:T(4,128)S(1)}, u32[]{:S(2)}, u32[]{:S(2)}) async-start(f32[32,4,16]{2,1,0:T(4,128)} %broadcast_in_dim.19), calls=%async_computation | async-start | bytes 131072 | tf_op jit(solution)/shard_map/all_to_all | solution.py:25
  235.2 11.0 %all-to-all-start.3 = ((f32[8,1,1]{2,1,0:T(1,128)}), f32[8,1,1]{2,1,0:T(1,128)S(1)}, u32[]{:S(2)}, u32[]{:S(2)}) async-start(f32[8,1,1]{2,1,0:T(1,128)} %broadcast_in_dim.22), calls=%async_computation.3 | async-start | bytes 8192 | tf_op jit(solution)/shard_map/all_to_all | solution.py:25
  246.2 8.6 %all-to-all-start.1 = ((f32[8,1,192]{2,1,0:T(1,128)}), f32[8,1,192]{2,1,0:T(1,128)S(1)}, u32[]{:S(2)}, u32[]{:S(2)}) async-start(f32[8,1,192]{2,1,0:T(1,128)} %reshape.61), calls=%async_computation.1 | async-start | bytes 16384 | tf_op jit(solution)/shard_map/all_to_all | solution.py:41
  256.1 12.3 %all-to-all-start.4 = ((f32[32,1,1]{2,1,0:T(1,128)}), f32[32,1,1]{2,1,0:T(1,128)S(1)}, u32[]{:S(2)}, u32[]{:S(2)}) async-start(f32[32,1,1]{2,1,0:T(1,128)} %broadcast_in_dim.40), calls=%async_computation.4 | async-start | bytes 32768 | tf_op jit(solution)/shard_map/all_to_all | solution.py:25
  268.3 12.5 %all-to-all-start.2 = ((f32[32,3,2]{1,2,0:T(2,128)}), f32[32,3,2]{1,2,0:T(2,128)S(1)}, u32[]{:S(2)}, u32[]{:S(2)}) async-start(f32[32,3,2]{1,2,0:T(2,128)} %copy.21), calls=%async_computation.2 | async-start | bytes 65536 | tf_op jit(solution)/shard_map/all_to_all | solution.py:49
where the time goes:
time: 284 us; the launch traced here: 283 us
  matrix products  183 us (64%)
  local copies, waits for them, and re-layouts  31 us (11%)
  starting transfers between devices  30 us (11%)
  waiting for transfers between devices  28.6 us (10%)
  other arithmetic  5.61 us (2%)
    dot_general x32, matrix products, gather_step(): jnp.dot(sine, all_charge, precision=lax.Precision.HIGHEST) * scale  63.4 us
    dot_general x32, matrix products, gather_step(): jnp.dot(cosine, all_charge, precision=lax.Precision.HIGHEST) * scale  40 us
    dot_general x32, matrix products, force_terms(): jnp.dot(grad_cosine, cosine, precision=lax.Precision.HIGHEST)  39.8 us
    dot_general x32, matrix products, force_terms(): jnp.dot(grad_sine, sine, precision=lax.Precision.HIGHEST)  39.3 us
    dynamic_update_slice x32, local copies, waits for them, and re-layouts, local(): lax.scan(gather_step, jnp.zeros((3, nsites_all), jnp.float32), (my_blocks...  24.2 us
    all_to_all x3, starting transfers between devices, from_everyone(): lax.all_to_all(jnp.broadcast_to(array[None], (peers, *array.shape)), axis...  22.2 us
    all_to_all x3, waiting for transfers between devices, from_everyone(): lax.all_to_all(jnp.broadcast_to(array[None], (peers, *array.shape)), axis...  17.2 us
    all_to_all x1, waiting for transfers between devices, summed_rows(): lax.all_to_all(nearer, far, split_axis=0, concat_axis=0, tiled=True)  7.35 us
  transfers between devices with their start and end apart: 5, of which 5 were waited for; matrix products, arithmetic and copies ran while one was open for 2% of the time, Pallas kernels for 0%

commit v1 on v0

v1 whole, which is shorter than its diff:
```python
import functools
import math

import jax
import jax.numpy as jnp
from jax import lax
from jax.experimental import pallas as pl
from jax.experimental.pallas import tpu as pltpu
from jax.sharding import Mesh
from jax.sharding import PartitionSpec as P

MMAX = 80
NCLS = 4
SITE = ("site_0", "site_1")
KA = ("ka_0", "ka_1")
SITE_KA = ("site_0", "site_1", "ka_0", "ka_1")
AXES = SITE_KA
MESH = pl.DeviceIdType.MESH
BLOCK = 256
LANES = 128
GROUP = 16
SINE = (4.442840086703501, -7.306690622039078, 3.589268246765133, -0.7724978545428361)


def offsets(far, near):
    steps = [(a, b) for a in range(far) for b in range(near)]
    return sorted(steps, key=lambda s: (min(s[0], far - s[0]) + min(s[1], near - s[1]), s))


def rounded(value):
    return value.astype(jnp.bfloat16).astype(jnp.float32)


def three_parts(value):
    high = rounded(value)
    middle = rounded(value - high)
    return high, middle, value - high - middle


def kernel(
    sizes,
    kvecs_all,
    positions,
    site_class,
    class_charge,
    miller,
    forces,
    energy,
    mints,
    xrows,
    columns,
    weight,
    table,
    angle,
    cosine,
    sine,
    creal,
    cimag,
    outbox,
    inbox,
    shared,
    mine_sem,
    site_send,
    site_recv,
    force_send,
    force_recv,
    last_send,
    last_recv,
):
    nz, ny, nx, nc = sizes
    kvecs = mints.shape[1]
    blocks = kvecs // BLOCK
    slots = offsets(nz, ny)
    mates = offsets(nx, nc)
    chunks = len(slots) // 8
    nsites = len(slots) * GROUP
    z, y, x, c = (lax.axis_index(axis) for axis in AXES)

    def at(dz, dy, dx, dc):
        return (lax.rem(z + dz, nz), lax.rem(y + dy, ny), lax.rem(x + dx, nx), lax.rem(c + dc, nc))

    start = pl.multiple_of((z * ny + y) * kvecs, LANES)
    fetch = pltpu.make_async_copy(miller.at[:, pl.ds(start, kvecs)], mints, mine_sem)
    fetch.start()
    barrier = pltpu.get_barrier_semaphore()
    for dz, dy in slots[1:]:
        pl.semaphore_signal(barrier, inc=1, device_id=at(dz, dy, 0, 0), device_id_type=MESH)
    for dx, dc in mates[1:]:
        pl.semaphore_signal(barrier, inc=1, device_id=at(0, 0, dx, dc), device_id_type=MESH)

    classes = site_class[...]
    charge = jnp.zeros(classes.shape, jnp.float32)
    for index in range(NCLS):
        charge = jnp.where(classes == index, class_charge[index], charge)
    place = positions[...]
    place = place - jnp.round(place)
    table[0] = jnp.concatenate(
        [place[0:1], place[1:2], place[2:3], charge, jnp.zeros((1, LANES - 4 * GROUP), jnp.float32)], axis=1
    )

    fetch.wait()
    limit = float(MMAX * MMAX)

    def prepare(block, carry):
        here = pl.ds(pl.multiple_of(block * BLOCK, BLOCK), BLOCK)
        m = mints[:, here].astype(jnp.float32)
        square = m[0:1] * m[0:1] + m[1:2] * m[1:2] + m[2:3] * m[2:3]
        w = limit * jnp.exp(-square / limit) / square
        rows = jnp.concatenate([m, m, m, *three_parts(w), jnp.zeros((4, BLOCK), jnp.float32)], axis=0)
        xrows[:, here] = rows.astype(jnp.bfloat16)
        columns[here, :] = rows.T.astype(jnp.bfloat16)
        return carry

    lax.fori_loop(0, blocks, prepare, 0)
    row = lax.broadcasted_iota(jnp.int32, (16, LANES), 0)
    picks = jnp.where((row >= 9) & (row < 12), 1.0, 0.0).astype(jnp.bfloat16)

    def spread(block, carry):
        here = pl.ds(pl.multiple_of(block * BLOCK, BLOCK), BLOCK)
        weight[here, :] = jnp.dot(columns[here, :], picks, preferred_element_type=jnp.float32)
        return carry

    lax.fori_loop(0, blocks, spread, 0)

    pl.semaphore_wait(barrier, len(slots) + len(mates) - 2)
    sends = [None]
    for slot, (dz, dy) in enumerate(slots):
        if slot:
            copy = pltpu.make_async_remote_copy(
                src_ref=table.at[0],
                dst_ref=table.at[slot],
                send_sem=site_send.at[slot],
                recv_sem=site_recv.at[slot],
                device_id=at(dz, dy, 0, 0),
                device_id_type=MESH,
            )
            copy.start()
            sends.append(copy)

    lane = lax.broadcasted_iota(jnp.int32, (8, LANES), 1)
    sublane = lax.broadcasted_iota(jnp.int32, (8, LANES), 0)
    group = lane // GROUP

    def unpack(chunk):
        got = table[pl.ds(8 * chunk, 8), 0, :]
        rolled = [got if r == 0 else pltpu.roll(got, GROUP * r, axis=1) for r in range(8)]
        out = []
        for d in range(4):
            value = jnp.zeros((8, LANES), jnp.float32)
            for s in range(8):
                value = jnp.where((sublane == s) & (group == s), rolled[(s - d) % 8], value)
            out.append(jnp.sum(value, axis=0, keepdims=True))
        coords = jnp.concatenate(out[:3], axis=0)
        parts = jnp.concatenate([*three_parts(coords), jnp.zeros((7, LANES), jnp.float32)], axis=0)
        return parts.astype(jnp.bfloat16), out[3]

    def angles(block, parts):
        here = pl.ds(pl.multiple_of(block * BLOCK, BLOCK), BLOCK)
        return jnp.dot(columns[here, :], parts, preferred_element_type=jnp.float32)

    def phase_one(chunk, parts, charges, first, last):
        half, lanes = chunk // 2, pl.ds((chunk % 2) * LANES, LANES)
        angle[0] = angles(0, parts)

        def step(block, total):
            following = angles(lax.rem(block + 1, blocks), parts)
            slot = lax.rem(block, 2)
            base = block * BLOCK
            for sub in range(BLOCK // 64):
                here = pl.ds(pl.multiple_of(base + sub * 64, 64), 64)
                turns = angle[slot, pl.ds(sub * 64, 64), :]
                f = turns - jnp.round(turns)
                f2 = f * f
                s = f * (SINE[0] + f2 * (SINE[1] + f2 * (SINE[2] + f2 * SINE[3])))
                p = s * s
                v = 2.0 - p
                co = 1.0 - p
                si = s * (v * lax.rsqrt(v))
                cosine[half, here, lanes] = co
                sine[half, here, lanes] = si
                re, im = charges * co, charges * si
                if not first:
                    re, im = creal[here, :] + re, cimag[here, :] + im
                if last:
                    re = jnp.sum(re, axis=1, keepdims=True)
                    im = jnp.sum(im, axis=1, keepdims=True)
                    w = weight[here, :]
                    wre, wim = w * re, w * im
                    e = wre * re + wim * im
                    for part in range(8):
                        total = total + e[8 * part : 8 * part + 8]
                    re, im = wre, wim
                creal[here, :] = re
                cimag[here, :] = im
            angle[1 - slot] = following
            return total

        return lax.fori_loop(0, blocks, step, jnp.zeros((8, LANES), jnp.float32))

    all_charges = []
    for chunk in range(chunks):
        for slot in range(8 * chunk, 8 * chunk + 8):
            if slot:
                sends[slot].wait_recv()
        parts, charges = unpack(chunk)
        all_charges.append(charges)
        total = phase_one(chunk, parts, charges, chunk == 0, chunk == chunks - 1)
    energy_row = jnp.sum(total, axis=0, keepdims=True) * (1.0 / (nsites * kvecs_all))
    scale = 4.0 * math.pi / math.sqrt(nsites * kvecs_all) / math.sqrt(nsites)

    posts = [None] * len(slots)
    for half in range(chunks // 2 - 1, -1, -1):

        def gather(block, total):
            here = pl.ds(pl.multiple_of(block * BLOCK, BLOCK), BLOCK)
            re, im = creal[here, :], cimag[here, :]
            parts = []
            for side in range(2):
                lanes = pl.ds(side * LANES, LANES)
                parts.append(sine[half, here, lanes] * re - cosine[half, here, lanes] * im)
            g = jnp.concatenate(parts, axis=1)
            high = g.astype(jnp.bfloat16)
            low = (g - high.astype(jnp.float32)).astype(jnp.bfloat16)
            m = xrows[:, here]
            return (
                total
                + jnp.dot(m, high, preferred_element_type=jnp.float32)
                + jnp.dot(m, low, preferred_element_type=jnp.float32)
            )

        force = lax.fori_loop(0, blocks, gather, jnp.zeros((16, 2 * LANES), jnp.float32), unroll=4)
        for side in (1, 0):
            chunk = 2 * half + side
            mine = force[0:3, side * LANES : (side + 1) * LANES] * (all_charges[chunk] * scale)
            outbox[chunk] = jnp.concatenate([mine, energy_row], axis=0)
        for side in (1, 0):
            chunk = 2 * half + side
            for slot in range(8 * chunk + 7, 8 * chunk - 1, -1):
                if slot == 0:
                    continue
                dz, dy = slots[slot]
                copy = pltpu.make_async_remote_copy(
                    src_ref=outbox.at[chunk],
                    dst_ref=inbox.at[slot],
                    send_sem=force_send.at[slot],
                    recv_sem=force_recv.at[slot],
                    device_id=at(nz - dz, ny - dy, 0, 0),
                    device_id_type=MESH,
                )
                copy.start()
                posts[slot] = copy

    row4 = lax.broadcasted_iota(jnp.int32, (4, LANES), 0)
    lane4 = lax.broadcasted_iota(jnp.int32, (4, LANES), 1)
    picked = jnp.zeros((4, LANES), jnp.float32)
    for s in range(8):
        own = None
        for chunk in range(chunks):
            slot = 8 * chunk + s
            if slot:
                posts[slot].wait_recv()
            value = inbox[slot] if slot else outbox[0]
            own = value if own is None else own + value
        picked = picked + jnp.where((row4 == 3) | (lane4 // GROUP == s), own, 0.0)
    shared[0] = picked
    lasts = []
    for mate, (dx, dc) in enumerate(mates):
        if mate:
            copy = pltpu.make_async_remote_copy(
                src_ref=shared.at[0],
                dst_ref=shared.at[mate],
                send_sem=last_send.at[mate],
                recv_sem=last_recv.at[mate],
                device_id=at(0, 0, dx, dc),
                device_id_type=MESH,
            )
            copy.start()
            lasts.append(copy)
    for copy in lasts:
        copy.wait_recv()
    whole = jnp.sum(shared[...], axis=0)
    per = forces.shape[1]
    mine = (x * nc + c) * per
    spot = lane4 % GROUP
    column = lax.broadcasted_iota(jnp.int32, (4, per), 1)
    out = jnp.zeros((4, per), jnp.float32)
    for index in range(per):
        value = jnp.sum(jnp.where(spot == mine + index, whole, 0.0), axis=1, keepdims=True)
        out = jnp.where(column == index, value, out)
    forces[...] = out[0:3]
    energy[...] = whole[3:4, 0:1]
    for copy in sends[1:] + posts[1:] + lasts:
        copy.wait_send()


def local(sizes, positions, site_class, class_charge, miller):
    nz, ny, nx, nc = sizes
    nslots, nmates = nz * ny, nx * nc
    kvecs = miller.shape[1] // nslots
    halves = nslots // 16
    vmem = pl.BlockSpec(memory_space=pltpu.VMEM)
    f32, bf16 = jnp.float32, jnp.bfloat16
    forces, energy = pl.pallas_call(
        functools.partial(kernel, sizes, miller.shape[1] * nmates),
        out_shape=(
            jax.ShapeDtypeStruct((3, positions.shape[1] // nmates), f32),
            jax.ShapeDtypeStruct((1, 1), f32),
        ),
        in_specs=[vmem, vmem, pl.BlockSpec(memory_space=pltpu.SMEM), pl.BlockSpec(memory_space=pl.ANY)],
        out_specs=(vmem, vmem),
        scratch_shapes=[
            pltpu.VMEM((3, kvecs), jnp.int32),
            pltpu.VMEM((16, kvecs), bf16),
            pltpu.VMEM((kvecs, 16), bf16),
            pltpu.VMEM((kvecs, LANES), f32),
            pltpu.VMEM((nslots, 1, LANES), f32),
            pltpu.VMEM((2, BLOCK, LANES), f32),
            pltpu.VMEM((halves, kvecs, 2 * LANES), f32),
            pltpu.VMEM((halves, kvecs, 2 * LANES), f32),
            pltpu.VMEM((kvecs, LANES), f32),
            pltpu.VMEM((kvecs, LANES), f32),
            pltpu.VMEM((nslots // 8, 4, LANES), f32),
            pltpu.VMEM((nslots, 4, LANES), f32),
            pltpu.VMEM((nmates, 4, LANES), f32),
            pltpu.SemaphoreType.DMA,
            pltpu.SemaphoreType.DMA((nslots,)),
            pltpu.SemaphoreType.DMA((nslots,)),
            pltpu.SemaphoreType.DMA((nslots,)),
            pltpu.SemaphoreType.DMA((nslots,)),
            pltpu.SemaphoreType.DMA((nmates,)),
            pltpu.SemaphoreType.DMA((nmates,)),
        ],
        compiler_params=pltpu.CompilerParams(
            collective_id=0, has_side_effects=True, vmem_limit_bytes=56 * 1024 * 1024
        ),
        name="ewald",
    )(positions, site_class.reshape(1, -1), class_charge, miller)
    return forces, energy.reshape(())


def solution(mesh):
    sizes = (8, 4, 4, 2)
    torus = Mesh(mesh.devices.reshape(sizes), AXES)
    placed = (P(None, SITE), P(SITE), P(), P(None, KA))
    return jax.shard_map(
        functools.partial(local, sizes),
        mesh=torus,
        in_specs=placed,
        out_specs=(P(None, SITE_KA), P()),
        check_vma=False,
    )
```

time: 284 us -> 45.2 us (0.16)
  matrix products: 183 us -> 0 us
  Pallas kernels: 0 us -> 41.3 us
  starting transfers between devices: 30 us -> 0 us
  local copies, waits for them, and re-layouts: 31 us -> 1.31 us
  waiting for transfers between devices: 28.6 us -> 0 us
  other arithmetic: 5.61 us -> 0 us
    dot_general x129 -> x0, matrix products: 183 us -> none  [the longest x32 63.4 us: gather_step(): jnp.dot(sine, all_charge, precision=lax.Precision.HIGHEST) * scale]
    pallas_call x0 -> x1, Pallas kernels: none -> 41.3 us  [local(): pl.pallas_call(functools.partial(kernel, sizes, miller.shape[1] * nmates)...]
    all_to_all x5 -> x0, starting transfers between devices: 30 us -> none  [the longest x3 22.2 us: from_everyone(): lax.all_to_all(jnp.broadcast_to(array[None], (peers, *array.shape)), axis...]
    all_to_all x5 -> x0, waiting for transfers between devices: 28.6 us -> none  [the longest x3 17.2 us: from_everyone(): lax.all_to_all(jnp.broadcast_to(array[None], (peers, *array.shape)), axis...]
    dynamic_update_slice x32 -> x0, local copies, waits for them, and re-layouts: 24.2 us -> none  [local(): lax.scan(gather_step, jnp.zeros((3, nsites_all), jnp.float32), (my_blocks...]
    reduce_sum x6 -> x0, other arithmetic: 3.36 us -> none  [the longest x2 1.24 us: over_copies(): return jnp.sum(everything, axis=0)]
    broadcast_in_dim x3 -> x0, local copies, waits for them, and re-layouts: 3.12 us -> none  [from_everyone(): jnp.broadcast_to(array[None], (peers, *array.shape))]
  transfers between devices with their start and end apart: 5 -> 0, of which waited for: 5 -> 0; matrix products, arithmetic and copies ran while one was open for 2% -> 0% of each run, Pallas kernels for 0% -> 0%
where the time goes in v1:
time: 45.2 us; the launch traced here: 45 us
  Pallas kernels  41.3 us (91%)
  between operations  2.4 us (5%)
  local copies, waits for them, and re-layouts  1.31 us (3%)
    pallas_call x1, Pallas kernels, local(): pl.pallas_call(functools.partial(kernel, sizes, miller.shape[1] * nmates)...  41.3 us
    unnamed x1, local copies, waits for them, and re-layouts  1.31 us

profile of v1, /device:TPU:1, one launch (start us, length us, event | category | flops | bytes accessed | tf_op | source)
XLA Modules:
  0.0 45.0 jit_solution(8670469571661359341)
XLA Ops:
  0.6 41.3 %ewald.1 = (f32[3,2]{1,0:T(4,128)}, f32[1,1]{1,0:T(1,128)}) custom-call(f32[3,16]{1,0:T(4,128)} %positions.1, s32[1,16]{1,0:T(1,128)} %bitcast.2, f32[4]{0:T(128)} %class_charge.1, s32[3,131072]{1,0:T(4,128)} %miller.1), custom_call_target="tpu_custom_call" | custom-call | tf_op jit(solution)/shard_map/ewald/pallas_call | solution.py:303
  42.0 1.3 %copy.6 = f32[3,2]{0,1:T(2,128)} copy(f32[3,2]{1,0:T(4,128)} %get-tuple-element.6) | data formatting | bytes 48

commit v2 on v1

--- a/solution.py
+++ b/solution.py
@@ -17,6 +17,7 @@
 AXES = SITE_KA
 MESH = pl.DeviceIdType.MESH
 BLOCK = 256
+STRIDE = 1024
 LANES = 128
 GROUP = 16
 SINE = (4.442840086703501, -7.306690622039078, 3.589268246765133, -0.7724978545428361)
@@ -83,7 +84,7 @@
     fetch = pltpu.make_async_copy(miller.at[:, pl.ds(start, kvecs)], mints, mine_sem)
     fetch.start()
     barrier = pltpu.get_barrier_semaphore()
-    for dz, dy in slots[1:]:
+    for dz, dy in slots[:0:-1]:
         pl.semaphore_signal(barrier, inc=1, device_id=at(dz, dy, 0, 0), device_id_type=MESH)
     for dx, dc in mates[1:]:
         pl.semaphore_signal(barrier, inc=1, device_id=at(0, 0, dx, dc), device_id_type=MESH)
@@ -98,6 +99,20 @@
         [place[0:1], place[1:2], place[2:3], charge, jnp.zeros((1, LANES - 4 * GROUP), jnp.float32)], axis=1
     )
 
+    pl.semaphore_wait(barrier, len(slots) + len(mates) - 2)
+    sends = [None] * len(slots)
+    for slot in range(len(slots) - 1, 0, -1):
+        dz, dy = slots[slot]
+        sends[slot] = pltpu.make_async_remote_copy(
+            src_ref=table.at[0],
+            dst_ref=table.at[slot],
+            send_sem=site_send.at[slot],
+            recv_sem=site_recv.at[slot],
+            device_id=at(dz, dy, 0, 0),
+            device_id_type=MESH,
+        )
+        sends[slot].start()
+
     fetch.wait()
     limit = float(MMAX * MMAX)
 
@@ -121,21 +136,6 @@
         return carry
 
     lax.fori_loop(0, blocks, spread, 0)
-
-    pl.semaphore_wait(barrier, len(slots) + len(mates) - 2)
-    sends = [None]
-    for slot, (dz, dy) in enumerate(slots):
-        if slot:
-            copy = pltpu.make_async_remote_copy(
-                src_ref=table.at[0],
-                dst_ref=table.at[slot],
-                send_sem=site_send.at[slot],
-                recv_sem=site_recv.at[slot],
-                device_id=at(dz, dy, 0, 0),
-                device_id_type=MESH,
-            )
-            copy.start()
-            sends.append(copy)
 
     lane = lax.broadcasted_iota(jnp.int32, (8, LANES), 1)
     sublane = lax.broadcasted_iota(jnp.int32, (8, LANES), 0)
@@ -154,8 +154,10 @@
         parts = jnp.concatenate([*three_parts(coords), jnp.zeros((7, LANES), jnp.float32)], axis=0)
         return parts.astype(jnp.bfloat16), out[3]
 
+    strides = kvecs // STRIDE
+
     def angles(block, parts):
-        here = pl.ds(pl.multiple_of(block * BLOCK, BLOCK), BLOCK)
+        here = pl.ds(pl.multiple_of(block * STRIDE, STRIDE), STRIDE)
         return jnp.dot(columns[here, :], parts, preferred_element_type=jnp.float32)
 
     def phase_one(chunk, parts, charges, first, last):
@@ -163,10 +165,10 @@
         angle[0] = angles(0, parts)
 
         def step(block, total):
-            following = angles(lax.rem(block + 1, blocks), parts)
+            following = angles(lax.rem(block + 1, strides), parts)
             slot = lax.rem(block, 2)
-            base = block * BLOCK
-            for sub in range(BLOCK // 64):
+            base = block * STRIDE
+            for sub in range(STRIDE // 64):
                 here = pl.ds(pl.multiple_of(base + sub * 64, 64), 64)
                 turns = angle[slot, pl.ds(sub * 64, 64), :]
                 f = turns - jnp.round(turns)
@@ -195,7 +197,7 @@
             angle[1 - slot] = following
             return total
 
-        return lax.fori_loop(0, blocks, step, jnp.zeros((8, LANES), jnp.float32))
+        return lax.fori_loop(0, strides, step, jnp.zeros((8, LANES), jnp.float32))
 
     all_charges = []
     for chunk in range(chunks):
@@ -228,7 +230,7 @@
                 + jnp.dot(m, low, preferred_element_type=jnp.float32)
             )
 
-        force = lax.fori_loop(0, blocks, gather, jnp.zeros((16, 2 * LANES), jnp.float32), unroll=4)
+        force = lax.fori_loop(0, blocks, gather, jnp.zeros((16, 2 * LANES), jnp.float32), unroll=True)
         for side in (1, 0):
             chunk = 2 * half + side
             mine = force[0:3, side * LANES : (side + 1) * LANES] * (all_charges[chunk] * scale)
@@ -250,6 +252,8 @@
                 copy.start()
                 posts[slot] = copy
 
+    for copy in sends[1:]:
+        copy.wait_send()
     row4 = lax.broadcasted_iota(jnp.int32, (4, LANES), 0)
     lane4 = lax.broadcasted_iota(jnp.int32, (4, LANES), 1)
     picked = jnp.zeros((4, LANES), jnp.float32)
@@ -276,20 +280,21 @@
             )
             copy.start()
             lasts.append(copy)
+    for copy in posts[1:]:
+        copy.wait_send()
     for copy in lasts:
         copy.wait_recv()
     whole = jnp.sum(shared[...], axis=0)
-    per = forces.shape[1]
+    per = forces.shape[0]
     mine = (x * nc + c) * per
     spot = lane4 % GROUP
-    column = lax.broadcasted_iota(jnp.int32, (4, per), 1)
-    out = jnp.zeros((4, per), jnp.float32)
+    out = []
     for index in range(per):
         value = jnp.sum(jnp.where(spot == mine + index, whole, 0.0), axis=1, keepdims=True)
-        out = jnp.where(column == index, value, out)
-    forces[...] = out[0:3]
+        out.append(jnp.sum(jnp.where(lane4 == row4, value, 0.0), axis=0, keepdims=True))
+    forces[...] = jnp.concatenate(out, axis=0)[:, 0:3]
     energy[...] = whole[3:4, 0:1]
-    for copy in sends[1:] + posts[1:] + lasts:
+    for copy in lasts:
         copy.wait_send()
 
 
@@ -303,7 +308,7 @@
     forces, energy = pl.pallas_call(
         functools.partial(kernel, sizes, miller.shape[1] * nmates),
         out_shape=(
-            jax.ShapeDtypeStruct((3, positions.shape[1] // nmates), f32),
+            jax.ShapeDtypeStruct((positions.shape[1] // nmates, 3), f32),
             jax.ShapeDtypeStruct((1, 1), f32),
         ),
         in_specs=[vmem, vmem, pl.BlockSpec(memory_space=pltpu.SMEM), pl.BlockSpec(memory_space=pl.ANY)],
@@ -314,7 +319,7 @@
             pltpu.VMEM((kvecs, 16), bf16),
             pltpu.VMEM((kvecs, LANES), f32),
             pltpu.VMEM((nslots, 1, LANES), f32),
-            pltpu.VMEM((2, BLOCK, LANES), f32),
+            pltpu.VMEM((2, STRIDE, LANES), f32),
             pltpu.VMEM((halves, kvecs, 2 * LANES), f32),
             pltpu.VMEM((halves, kvecs, 2 * LANES), f32),
             pltpu.VMEM((kvecs, LANES), f32),
@@ -335,7 +340,7 @@
         ),
         name="ewald",
     )(positions, site_class.reshape(1, -1), class_charge, miller)
-    return forces, energy.reshape(())
+    return forces.T, energy.reshape(())
 
 
 def solution(mesh):

time: 45.2 us -> 43.2 us (0.956)
  Pallas kernels: 41.3 us -> 39.5 us
    pallas_call x1, Pallas kernels: 41.3 us -> 39.5 us  [local(): pl.pallas_call(functools.partial(kernel, sizes, miller.shape[1] * nmates)...]
where the time goes in v2:
time: 43.2 us; the launch traced here: 43.1 us
  Pallas kernels  39.5 us (91%)
  between operations  2.4 us (6%)
  local copies, waits for them, and re-layouts  1.22 us (3%)
    pallas_call x1, Pallas kernels, local(): pl.pallas_call(functools.partial(kernel, sizes, miller.shape[1] * nmates)...  39.5 us
    unnamed x1, local copies, waits for them, and re-layouts  1.22 us

profile of v2, /device:TPU:1, one launch (start us, length us, event | category | flops | bytes accessed | tf_op | source)
XLA Modules:
  0.0 43.1 jit_solution(11019913869868701818)
XLA Ops:
  0.6 39.5 %ewald.1 = (f32[2,3]{1,0:T(2,128)}, f32[1,1]{1,0:T(1,128)}) custom-call(f32[3,16]{1,0:T(4,128)} %positions.1, s32[1,16]{1,0:T(1,128)} %bitcast.4, f32[4]{0:T(128)} %class_charge.1, s32[3,131072]{1,0:T(4,128)} %miller.1), custom_call_target="tpu_custom_call" | custom-call | tf_op jit(solution)/shard_map/ewald/pallas_call | solution.py:308
  40.1 1.2 %copy.8 = f32[3,2]{0,1:T(2,128)} copy(f32[3,2]{0,1:T(2,128)} %bitcast.3) | data formatting | bytes 48

commit v3 on v2

v3 whole, which is shorter than its diff:
```python
import functools
import math

import jax
import jax.numpy as jnp
from jax import lax
from jax.experimental import pallas as pl
from jax.experimental.pallas import tpu as pltpu
from jax.sharding import Mesh
from jax.sharding import PartitionSpec as P

MMAX = 80
NCLS = 4
SITE = ("site_0", "site_1")
KA = ("ka_0", "ka_1")
SITE_KA = ("site_0", "site_1", "ka_0", "ka_1")
AXES = SITE_KA
MESH = pl.DeviceIdType.MESH
BLOCK = 256
STRIDE = 512
LANES = 128
GROUP = 16
SINE = (4.442840086703501, -7.306690622039078, 3.589268246765133, -0.7724978545428361)


def offsets(far, near):
    steps = [(a, b) for a in range(far) for b in range(near)]
    return sorted(steps, key=lambda s: (min(s[0], far - s[0]) + min(s[1], near - s[1]), s))


def rounded(value):
    return value.astype(jnp.bfloat16).astype(jnp.float32)


def three_parts(value):
    high = rounded(value)
    middle = rounded(value - high)
    return high, middle, value - high - middle


def kernel(
    sizes,
    positions,
    site_class,
    class_charge,
    miller,
    forces,
    energy,
    held_place,
    held_class,
    held_charge,
    mints,
    xrows,
    columns,
    weight,
    table,
    angle_a,
    angle_b,
    cosine,
    sine,
    creal,
    cimag,
    outbox,
    inbox,
    shared,
    mine_sem,
    site_send,
    site_recv,
    force_send,
    force_recv,
    last_send,
    last_recv,
):
    nz, ny, nx, nc = sizes
    kvecs = mints.shape[1]
    blocks = kvecs // BLOCK
    slots = offsets(nz, ny)
    mates = offsets(nx, nc)
    chunks = len(slots) // 8
    z, y, x, c = (lax.axis_index(axis) for axis in AXES)

    def at(dz, dy, dx, dc):
        return (lax.rem(z + dz, nz), lax.rem(y + dy, ny), lax.rem(x + dx, nx), lax.rem(c + dc, nc))

    barrier = pltpu.get_barrier_semaphore()
    for dz, dy in slots[:0:-1]:
        pl.semaphore_signal(barrier, inc=1, device_id=at(dz, dy, 0, 0), device_id_type=MESH)
    for dx, dc in mates[1:]:
        pl.semaphore_signal(barrier, inc=1, device_id=at(0, 0, dx, dc), device_id_type=MESH)
    start = pl.multiple_of((z * ny + y) * kvecs, LANES)
    fetches = [
        pltpu.make_async_copy(source, target, mine_sem.at[index])
        for index, (source, target) in enumerate(
            (
                (positions, held_place),
                (site_class, held_class),
                (class_charge, held_charge),
                (miller.at[:, pl.ds(start, kvecs)], mints),
            )
        )
    ]
    for fetch in fetches:
        fetch.start()
    for fetch in fetches[:3]:
        fetch.wait()

    classes = held_class[...]
    charge = jnp.zeros(classes.shape, jnp.float32)
    for index in range(NCLS):
        charge = jnp.where(classes == index, held_charge[index], charge)
    place = held_place[...]
    place = place - jnp.round(place)
    table[0] = jnp.concatenate(
        [place[0:1], place[1:2], place[2:3], charge, jnp.zeros((1, LANES - 4 * GROUP), jnp.float32)], axis=1
    )

    pl.semaphore_wait(barrier, len(slots) + len(mates) - 2)
    for slot in range(len(slots) - 1, 0, -1):
        dz, dy = slots[slot]
        pltpu.make_async_remote_copy(
            src_ref=table.at[0],
            dst_ref=table.at[slot],
            send_sem=site_send,
            recv_sem=site_recv.at[slot // 8],
            device_id=at(dz, dy, 0, 0),
            device_id_type=MESH,
        ).start()

    fetches[3].wait()
    limit = float(MMAX * MMAX)
    row = lax.broadcasted_iota(jnp.int32, (16, LANES), 0)
    picks = jnp.where((row >= 9) & (row < 12), 1.0, 0.0).astype(jnp.bfloat16)

    def prepare(block, carry):
        here = pl.ds(pl.multiple_of(block * BLOCK, BLOCK), BLOCK)
        m = mints[:, here].astype(jnp.float32)
        square = m[0:1] * m[0:1] + m[1:2] * m[1:2] + m[2:3] * m[2:3]
        w = limit * jnp.exp(-square / limit) / square
        rows = jnp.concatenate([m, m, m, *three_parts(w), jnp.zeros((4, BLOCK), jnp.float32)], axis=0)
        xrows[:, here] = rows.astype(jnp.bfloat16)
        turned = rows.T.astype(jnp.bfloat16)
        columns[here, :] = turned
        weight[here, :] = jnp.dot(turned, picks, preferred_element_type=jnp.float32)
        return carry

    lax.fori_loop(0, blocks, prepare, 0, unroll=True)

    lane = lax.broadcasted_iota(jnp.int32, (8, LANES), 1)
    sublane = lax.broadcasted_iota(jnp.int32, (8, LANES), 0)
    group = lane // GROUP

    def unpack(chunk):
        got = table[pl.ds(8 * chunk, 8), 0, :]
        rolled = [got if r == 0 else pltpu.roll(got, GROUP * r, axis=1) for r in range(8)]
        out = []
        for d in range(4):
            value = jnp.zeros((8, LANES), jnp.float32)
            for s in range(8):
                value = jnp.where((sublane == s) & (group == s), rolled[(s - d) % 8], value)
            out.append(jnp.sum(value, axis=0, keepdims=True))
        coords = jnp.concatenate(out[:3], axis=0)
        parts = jnp.concatenate([*three_parts(coords), jnp.zeros((7, LANES), jnp.float32)], axis=0)
        return parts.astype(jnp.bfloat16), out[3]

    strides = kvecs // STRIDE

    def angles(block, parts):
        here = pl.ds(pl.multiple_of(block * STRIDE, STRIDE), STRIDE)
        return jnp.dot(columns[here, :], parts, preferred_element_type=jnp.float32)

    def phase_one(chunk, parts, charges, first, last):
        half, lanes = chunk // 2, pl.ds((chunk % 2) * LANES, LANES)
        angle_a[...] = angles(0, parts)

        def process(angle, base, total):
            for sub in range(STRIDE // 64):
                here = pl.ds(pl.multiple_of(base + sub * 64, 64), 64)
                turns = angle[pl.ds(sub * 64, 64), :]
                f = turns - jnp.round(turns)
                f2 = f * f
                s = f * (SINE[0] + f2 * (SINE[1] + f2 * (SINE[2] + f2 * SINE[3])))
                p = s * s
                v = 2.0 - p
                co = 1.0 - p
                si = s * (v * lax.rsqrt(v))
                cosine[half, here, lanes] = co
                sine[half, here, lanes] = si
                re, im = charges * co, charges * si
                if not first:
                    re, im = creal[here, :] + re, cimag[here, :] + im
                if last:
                    re = jnp.sum(re, axis=1, keepdims=True)
                    im = jnp.sum(im, axis=1, keepdims=True)
                    w = weight[here, :]
                    wre, wim = w * re, w * im
                    e = wre * re + wim * im
                    for part in range(8):
                        total = total + e[8 * part : 8 * part + 8]
                    re, im = wre, wim
                creal[here, :] = re
                cimag[here, :] = im
            return total

        def step(pair, total):
            angle_b[...] = angles(2 * pair + 1, parts)
            total = process(angle_a, 2 * pair * STRIDE, total)
            angle_a[...] = angles(lax.rem(2 * pair + 2, strides), parts)
            return process(angle_b, (2 * pair + 1) * STRIDE, total)

        return lax.fori_loop(0, strides // 2, step, jnp.zeros((8, LANES), jnp.float32))

    def arrived(ref, chunk, sems):
        span = ref.at[pl.ds(max(8 * chunk, 1), 8 if chunk else 7)]
        pltpu.make_async_copy(span, span, sems.at[chunk]).wait()

    def departed(ref, sem):
        span = ref.at[pl.ds(1, ref.shape[0] - 1)]
        pltpu.make_async_copy(span, span, sem).wait()

    all_charges = []
    for chunk in range(chunks):
        arrived(table, chunk, site_recv)
        parts, charges = unpack(chunk)
        all_charges.append(charges)
        total = phase_one(chunk, parts, charges, chunk == 0, chunk == chunks - 1)
    energy_row = jnp.sum(total, axis=0, keepdims=True)

    for half in range(chunks // 2 - 1, -1, -1):

        def gather(block, total):
            here = pl.ds(pl.multiple_of(block * BLOCK, BLOCK), BLOCK)
            re, im = creal[here, :], cimag[here, :]
            parts = []
            for side in range(2):
                lanes = pl.ds(side * LANES, LANES)
                parts.append(sine[half, here, lanes] * re - cosine[half, here, lanes] * im)
            g = jnp.concatenate(parts, axis=1)
            high = g.astype(jnp.bfloat16)
            low = (g - high.astype(jnp.float32)).astype(jnp.bfloat16)
            m = xrows[:, here]
            return (
                total
                + jnp.dot(m, high, preferred_element_type=jnp.float32)
                + jnp.dot(m, low, preferred_element_type=jnp.float32)
            )

        force = lax.fori_loop(0, blocks, gather, jnp.zeros((16, 2 * LANES), jnp.float32), unroll=True)
        for side in (1, 0):
            chunk = 2 * half + side
            mine = force[0:3, side * LANES : (side + 1) * LANES] * all_charges[chunk]
            outbox[chunk] = jnp.concatenate([mine, energy_row], axis=0)
        for side in (1, 0):
            chunk = 2 * half + side
            for slot in range(8 * chunk + 7, 8 * chunk - 1, -1):
                if slot == 0:
                    continue
                dz, dy = slots[slot]
                pltpu.make_async_remote_copy(
                    src_ref=outbox.at[chunk],
                    dst_ref=inbox.at[slot],
                    send_sem=force_send,
                    recv_sem=force_recv.at[chunk],
                    device_id=at(nz - dz, ny - dy, 0, 0),
                    device_id_type=MESH,
                ).start()

    departed(table, site_send)
    row4 = lax.broadcasted_iota(jnp.int32, (4, LANES), 0)
    lane4 = lax.broadcasted_iota(jnp.int32, (4, LANES), 1)
    boxes = [None] * 8
    for chunk in range(chunks):
        arrived(inbox, chunk, force_recv)
        for s in range(8):
            value = inbox[8 * chunk + s] if chunk or s else outbox[0]
            boxes[s] = value if boxes[s] is None else boxes[s] + value
    picked = jnp.zeros((4, LANES), jnp.float32)
    for s in range(8):
        picked = picked + jnp.where((row4 == 3) | (lane4 // GROUP == s), boxes[s], 0.0)
    shared[0] = picked
    for mate in range(len(mates) - 1, 0, -1):
        dx, dc = mates[mate]
        pltpu.make_async_remote_copy(
            src_ref=shared.at[0],
            dst_ref=shared.at[mate],
            send_sem=last_send,
            recv_sem=last_recv,
            device_id=at(0, 0, dx, dc),
            device_id_type=MESH,
        ).start()
    departed(inbox, force_send)
    departed(shared, last_recv)
    whole = jnp.sum(shared[...], axis=0)
    per = forces.shape[0]
    mine = (x * nc + c) * per
    spot = lane4 % GROUP
    out = []
    for index in range(per):
        value = jnp.sum(jnp.where(spot == mine + index, whole, 0.0), axis=1, keepdims=True)
        out.append(jnp.sum(jnp.where(lane4 == row4, value, 0.0), axis=0, keepdims=True))
    forces[...] = jnp.concatenate(out, axis=0)[:, 0:3]
    energy[...] = whole[3:4, 0:1]
    departed(shared, last_send)


def local(sizes, positions, site_class, class_charge, miller):
    nz, ny, nx, nc = sizes
    nslots, nmates = nz * ny, nx * nc
    kvecs = miller.shape[1] // nslots
    halves = nslots // 16
    vmem = pl.BlockSpec(memory_space=pltpu.VMEM)
    f32, bf16 = jnp.float32, jnp.bfloat16
    forces, energy = pl.pallas_call(
        functools.partial(kernel, sizes),
        out_shape=(
            jax.ShapeDtypeStruct((positions.shape[1] // nmates, 3), f32),
            jax.ShapeDtypeStruct((1, 1), f32),
        ),
        in_specs=[pl.BlockSpec(memory_space=pl.ANY)] * 4,
        out_specs=(vmem, vmem),
        scratch_shapes=[
            pltpu.VMEM(positions.shape, f32),
            pltpu.VMEM((1, site_class.shape[0]), jnp.int32),
            pltpu.SMEM(class_charge.shape, f32),
            pltpu.VMEM((3, kvecs), jnp.int32),
            pltpu.VMEM((16, kvecs), bf16),
            pltpu.VMEM((kvecs, 16), bf16),
            pltpu.VMEM((kvecs, LANES), f32),
            pltpu.VMEM((nslots, 1, LANES), f32),
            pltpu.VMEM((STRIDE, LANES), f32),
            pltpu.VMEM((STRIDE, LANES), f32),
            pltpu.VMEM((halves, kvecs, 2 * LANES), f32),
            pltpu.VMEM((halves, kvecs, 2 * LANES), f32),
            pltpu.VMEM((kvecs, LANES), f32),
            pltpu.VMEM((kvecs, LANES), f32),
            pltpu.VMEM((nslots // 8, 4, LANES), f32),
            pltpu.VMEM((nslots, 4, LANES), f32),
            pltpu.VMEM((nmates, 4, LANES), f32),
            pltpu.SemaphoreType.DMA((4,)),
            pltpu.SemaphoreType.DMA,
            pltpu.SemaphoreType.DMA((nslots // 8,)),
            pltpu.SemaphoreType.DMA,
            pltpu.SemaphoreType.DMA((nslots // 8,)),
            pltpu.SemaphoreType.DMA,
            pltpu.SemaphoreType.DMA,
        ],
        compiler_params=pltpu.CompilerParams(
            collective_id=0, has_side_effects=True, vmem_limit_bytes=56 * 1024 * 1024
        ),
        name="ewald",
    )(positions, site_class.reshape(1, -1), class_charge, miller)
    nsites, kvecs_all = positions.shape[1] * nslots, miller.shape[1] * nmates
    scale = 4.0 * math.pi / math.sqrt(nsites * kvecs_all) / math.sqrt(nsites)
    return forces.T * scale, energy.reshape(()) * (1.0 / (nsites * kvecs_all))


def solution(mesh):
    sizes = (8, 4, 4, 2)
    torus = Mesh(mesh.devices.reshape(sizes), AXES)
    placed = (P(None, SITE), P(SITE), P(), P(None, KA))
    return jax.shard_map(
        functools.partial(local, sizes),
        mesh=torus,
        in_specs=placed,
        out_specs=(P(None, SITE_KA), P()),
        check_vma=False,
    )
```

time: 43.2 us -> 39.9 us (0.924)
  Pallas kernels: 39.5 us -> 36.2 us
  other arithmetic: 0 us -> 1.22 us
  local copies, waits for them, and re-layouts: 1.22 us -> 0 us
    pallas_call x1, Pallas kernels: 39.5 us -> 36.2 us  [local(): pl.pallas_call(functools.partial(kernel, sizes), out_shape=(jax.ShapeDtyp...]
    mul x0 -> x1, other arithmetic: none -> 1.22 us  [local(): return (forces.T * scale, energy.reshape(()) * (1.0 / (nsites * kvecs_all)))]
    unnamed x1 -> x0, local copies, waits for them, and re-layouts: 1.22 us -> none
where the time goes in v3:
time: 39.9 us; the launch traced here: 39.8 us
  Pallas kernels  36.2 us (91%)
  between operations  2.4 us (6%)
  other arithmetic  1.22 us (3%)
    pallas_call x1, Pallas kernels, local(): pl.pallas_call(functools.partial(kernel, sizes), out_shape=(jax.ShapeDtyp...  36.2 us
    mul x1, other arithmetic, local(): return (forces.T * scale, energy.reshape(()) * (1.0 / (nsites * kvecs_all)))  1.22 us

profile of v3, /device:TPU:1, one launch (start us, length us, event | category | flops | bytes accessed | tf_op | source)
XLA Modules:
  0.0 39.8 jit_solution(15835419953500418266)
XLA Ops:
  0.6 36.2 %ewald.1 = (f32[2,3]{1,0:T(2,128)}, f32[1,1]{1,0:T(1,128)}) custom-call(f32[3,16]{1,0:T(4,128)} %positions.1, s32[1,16]{1,0:T(1,128)} %bitcast.4, f32[4]{0:T(128)} %class_charge.1, s32[3,131072]{1,0:T(4,128)} %miller.1), custom_call_target="tpu_custom_call" | custom-call | tf_op jit(solution)/shard_map/ewald/pallas_call | solution.py:312
  37.4 1.2 %multiply_bitcast_fusion = f32[3,2]{0,1:T(2,128)} fusion(f32[2,3]{1,0:T(2,128)} %get-tuple-element.4), kind=kLoop, calls=%fused_computation | loop fusion | flops 6 | bytes 48 | tf_op jit(solution)/shard_map/mul | solution.py:353

commit v4 on v3

--- a/solution.py
+++ b/solution.py
@@ -17,10 +17,14 @@
 AXES = SITE_KA
 MESH = pl.DeviceIdType.MESH
 BLOCK = 256
-STRIDE = 512
+STRIDE = 4096
+ROWS = 128
+GROUPS = 3
 LANES = 128
 GROUP = 16
-SINE = (4.442840086703501, -7.306690622039078, 3.589268246765133, -0.7724978545428361)
+SINE = (0.7724978545428361, 0.9809405073019027, -3.66537433, 5.8630113)
+SHY = 1.0 - 5.0e-7
+TINY = 1.0e-30
 
 
 def offsets(far, near):
@@ -54,8 +58,6 @@
     columns,
     weight,
     table,
-    angle_a,
-    angle_b,
     cosine,
     sine,
     creal,
@@ -120,7 +122,7 @@
         pltpu.make_async_remote_copy(
             src_ref=table.at[0],
             dst_ref=table.at[slot],
-            send_sem=site_send,
+            send_sem=site_send.at[slot * 2 // len(slots)],
             recv_sem=site_recv.at[slot // 8],
             device_id=at(dz, dy, 0, 0),
             device_id_type=MESH,
@@ -136,7 +138,7 @@
         m = mints[:, here].astype(jnp.float32)
         square = m[0:1] * m[0:1] + m[1:2] * m[1:2] + m[2:3] * m[2:3]
         w = limit * jnp.exp(-square / limit) / square
-        rows = jnp.concatenate([m, m, m, *three_parts(w), jnp.zeros((4, BLOCK), jnp.float32)], axis=0)
+        rows = jnp.concatenate([m, m, m, *three_parts(w), jnp.ones((4, BLOCK), jnp.float32)], axis=0)
         xrows[:, here] = rows.astype(jnp.bfloat16)
         turned = rows.T.astype(jnp.bfloat16)
         columns[here, :] = turned
@@ -159,33 +161,30 @@
                 value = jnp.where((sublane == s) & (group == s), rolled[(s - d) % 8], value)
             out.append(jnp.sum(value, axis=0, keepdims=True))
         coords = jnp.concatenate(out[:3], axis=0)
-        parts = jnp.concatenate([*three_parts(coords), jnp.zeros((7, LANES), jnp.float32)], axis=0)
-        return parts.astype(jnp.bfloat16), out[3]
-
-    strides = kvecs // STRIDE
-
-    def angles(block, parts):
-        here = pl.ds(pl.multiple_of(block * STRIDE, STRIDE), STRIDE)
-        return jnp.dot(columns[here, :], parts, preferred_element_type=jnp.float32)
-
-    def phase_one(chunk, parts, charges, first, last):
+        flip = jnp.where(out[3] < 0.0, 0.5, 0.0)
+        none = jnp.zeros((3, LANES), jnp.float32)
+        parts = jnp.concatenate([*three_parts(coords), none, flip, none], axis=0)
+        size = jnp.maximum(jnp.abs(out[3]), TINY)
+        return parts.astype(jnp.bfloat16), size, (SINE[0] * SHY) * jnp.sqrt(size)
+
+    def phase_one(chunk, parts, size, amplitude, first, last):
         half, lanes = chunk // 2, pl.ds((chunk % 2) * LANES, LANES)
-        angle_a[...] = angles(0, parts)
-
-        def process(angle, base, total):
-            for sub in range(STRIDE // 64):
-                here = pl.ds(pl.multiple_of(base + sub * 64, 64), 64)
-                turns = angle[pl.ds(sub * 64, 64), :]
+        twice = 2.0 * size
+
+        def step(stride, total):
+            base = stride * STRIDE
+            for sub in range(STRIDE // ROWS):
+                here = pl.ds(pl.multiple_of(base + sub * ROWS, ROWS), ROWS)
+                turns = jnp.dot(columns[here, :], parts, preferred_element_type=jnp.float32)
                 f = turns - jnp.round(turns)
                 f2 = f * f
-                s = f * (SINE[0] + f2 * (SINE[1] + f2 * (SINE[2] + f2 * SINE[3])))
+                s = (amplitude * f) * ((SINE[1] - f2) * ((f2 + SINE[2]) * f2 + SINE[3]))
                 p = s * s
-                v = 2.0 - p
-                co = 1.0 - p
-                si = s * (v * lax.rsqrt(v))
-                cosine[half, here, lanes] = co
-                sine[half, here, lanes] = si
-                re, im = charges * co, charges * si
+                v = twice - p
+                re = size - p
+                im = s * (v * lax.rsqrt(v))
+                cosine[half, here, lanes] = re
+                sine[half, here, lanes] = im
                 if not first:
                     re, im = creal[here, :] + re, cimag[here, :] + im
                 if last:
@@ -194,47 +193,37 @@
                     w = weight[here, :]
                     wre, wim = w * re, w * im
                     e = wre * re + wim * im
-                    for part in range(8):
+                    for part in range(ROWS // 8):
                         total = total + e[8 * part : 8 * part + 8]
                     re, im = wre, wim
                 creal[here, :] = re
                 cimag[here, :] = im
             return total
 
-        def step(pair, total):
-            angle_b[...] = angles(2 * pair + 1, parts)
-            total = process(angle_a, 2 * pair * STRIDE, total)
-            angle_a[...] = angles(lax.rem(2 * pair + 2, strides), parts)
-            return process(angle_b, (2 * pair + 1) * STRIDE, total)
-
-        return lax.fori_loop(0, strides // 2, step, jnp.zeros((8, LANES), jnp.float32))
+        return lax.fori_loop(0, kvecs // STRIDE, step, jnp.zeros((8, LANES), jnp.float32))
 
     def arrived(ref, chunk, sems):
         span = ref.at[pl.ds(max(8 * chunk, 1), 8 if chunk else 7)]
         pltpu.make_async_copy(span, span, sems.at[chunk]).wait()
 
-    def departed(ref, sem):
-        span = ref.at[pl.ds(1, ref.shape[0] - 1)]
+    def departed(ref, sem, first, count):
+        span = ref.at[pl.ds(first, count)]
         pltpu.make_async_copy(span, span, sem).wait()
 
-    all_charges = []
     for chunk in range(chunks):
         arrived(table, chunk, site_recv)
-        parts, charges = unpack(chunk)
-        all_charges.append(charges)
-        total = phase_one(chunk, parts, charges, chunk == 0, chunk == chunks - 1)
+        total = phase_one(chunk, *unpack(chunk), chunk == 0, chunk == chunks - 1)
     energy_row = jnp.sum(total, axis=0, keepdims=True)
 
-    for half in range(chunks // 2 - 1, -1, -1):
-
+    def phase_two(group):
         def gather(block, total):
             here = pl.ds(pl.multiple_of(block * BLOCK, BLOCK), BLOCK)
             re, im = creal[here, :], cimag[here, :]
             parts = []
-            for side in range(2):
-                lanes = pl.ds(side * LANES, LANES)
+            for chunk in group:
+                half, lanes = chunk // 2, pl.ds((chunk % 2) * LANES, LANES)
                 parts.append(sine[half, here, lanes] * re - cosine[half, here, lanes] * im)
-            g = jnp.concatenate(parts, axis=1)
+            g = parts[0] if len(parts) == 1 else jnp.concatenate(parts, axis=1)
             high = g.astype(jnp.bfloat16)
             low = (g - high.astype(jnp.float32)).astype(jnp.bfloat16)
             m = xrows[:, here]
@@ -244,13 +233,10 @@
                 + jnp.dot(m, low, preferred_element_type=jnp.float32)
             )
 
-        force = lax.fori_loop(0, blocks, gather, jnp.zeros((16, 2 * LANES), jnp.float32), unroll=True)
-        for side in (1, 0):
-            chunk = 2 * half + side
-            mine = force[0:3, side * LANES : (side + 1) * LANES] * all_charges[chunk]
-            outbox[chunk] = jnp.concatenate([mine, energy_row], axis=0)
-        for side in (1, 0):
-            chunk = 2 * half + side
+        force = lax.fori_loop(0, blocks, gather, jnp.zeros((16, len(group) * LANES), jnp.float32), unroll=True)
+        for index, chunk in enumerate(group):
+            outbox[chunk] = jnp.concatenate([force[0:3, index * LANES : (index + 1) * LANES], energy_row], axis=0)
+        for chunk in group:
             for slot in range(8 * chunk + 7, 8 * chunk - 1, -1):
                 if slot == 0:
                     continue
@@ -264,7 +250,17 @@
                     device_id_type=MESH,
                 ).start()
 
-    departed(table, site_send)
+    if GROUPS == 3:
+        phase_two((3,))
+        departed(table, site_send.at[1], len(slots) // 2, len(slots) // 2)
+        phase_two((2,))
+        departed(table, site_send.at[0], 1, len(slots) // 2 - 1)
+        phase_two((1, 0))
+    else:
+        phase_two((3, 2))
+        departed(table, site_send.at[1], len(slots) // 2, len(slots) // 2)
+        departed(table, site_send.at[0], 1, len(slots) // 2 - 1)
+        phase_two((1, 0))
     row4 = lax.broadcasted_iota(jnp.int32, (4, LANES), 0)
     lane4 = lax.broadcasted_iota(jnp.int32, (4, LANES), 1)
     boxes = [None] * 8
@@ -287,8 +283,8 @@
             device_id=at(0, 0, dx, dc),
             device_id_type=MESH,
         ).start()
-    departed(inbox, force_send)
-    departed(shared, last_recv)
+    departed(inbox, force_send, 1, len(slots) - 1)
+    departed(shared, last_recv, 1, len(mates) - 1)
     whole = jnp.sum(shared[...], axis=0)
     per = forces.shape[0]
     mine = (x * nc + c) * per
@@ -299,7 +295,7 @@
         out.append(jnp.sum(jnp.where(lane4 == row4, value, 0.0), axis=0, keepdims=True))
     forces[...] = jnp.concatenate(out, axis=0)[:, 0:3]
     energy[...] = whole[3:4, 0:1]
-    departed(shared, last_send)
+    departed(shared, last_send, 1, len(mates) - 1)
 
 
 def local(sizes, positions, site_class, class_charge, miller):
@@ -312,8 +308,8 @@
     forces, energy = pl.pallas_call(
         functools.partial(kernel, sizes),
         out_shape=(
-            jax.ShapeDtypeStruct((positions.shape[1] // nmates, 3), f32),
-            jax.ShapeDtypeStruct((1, 1), f32),
+            pltpu.VMEM((positions.shape[1] // nmates, 3), f32),
+            pltpu.VMEM((1, 1), f32),
         ),
         in_specs=[pl.BlockSpec(memory_space=pl.ANY)] * 4,
         out_specs=(vmem, vmem),
@@ -326,8 +322,6 @@
             pltpu.VMEM((kvecs, 16), bf16),
             pltpu.VMEM((kvecs, LANES), f32),
             pltpu.VMEM((nslots, 1, LANES), f32),
-            pltpu.VMEM((STRIDE, LANES), f32),
-            pltpu.VMEM((STRIDE, LANES), f32),
             pltpu.VMEM((halves, kvecs, 2 * LANES), f32),
             pltpu.VMEM((halves, kvecs, 2 * LANES), f32),
             pltpu.VMEM((kvecs, LANES), f32),
@@ -336,7 +330,7 @@
             pltpu.VMEM((nslots, 4, LANES), f32),
             pltpu.VMEM((nmates, 4, LANES), f32),
             pltpu.SemaphoreType.DMA((4,)),
-            pltpu.SemaphoreType.DMA,
+            pltpu.SemaphoreType.DMA((2,)),
             pltpu.SemaphoreType.DMA((nslots // 8,)),
             pltpu.SemaphoreType.DMA,
             pltpu.SemaphoreType.DMA((nslots // 8,)),

time: 39.9 us -> 36.3 us (0.910)
  Pallas kernels: 36.2 us -> 33.3 us
  other arithmetic: 1.22 us -> 0.56 us
    pallas_call x1, Pallas kernels: 36.2 us -> 33.3 us  [local(): pl.pallas_call(functools.partial(kernel, sizes), out_shape=(pltpu.VMEM((p...]
    mul x1, other arithmetic: 1.22 us -> 0.56 us  [local(): return (forces.T * scale, energy.reshape(()) * (1.0 / (nsites * kvecs_all)))]
where the time goes in v4:
time: 36.3 us; the launch traced here: 36.1 us
  Pallas kernels  33.3 us (92%)
  between operations  2.33 us (6%)
  other arithmetic  0.56 us (2%)
    pallas_call x1, Pallas kernels, local(): pl.pallas_call(functools.partial(kernel, sizes), out_shape=(pltpu.VMEM((p...  33.3 us

profile of v4, /device:TPU:1, one launch (start us, length us, event | category | flops | bytes accessed | tf_op | source)
XLA Modules:
  0.0 36.1 jit_solution(12344494982149247660)
XLA Ops:
  0.6 33.3 %ewald.1 = (f32[2,3]{1,0:T(2,128)S(1)}, f32[1,1]{1,0:T(1,128)}) custom-call(f32[3,16]{1,0:T(4,128)} %positions.1, s32[1,16]{1,0:T(1,128)} %bitcast.4, f32[4]{0:T(128)} %class_charge.1, s32[3,131072]{1,0:T(4,128)} %miller.1), custom_call_target="tpu_custom_call" | custom-call | tf_op jit(solution)/shard_map/ewald/pallas_call | solution.py:308
  34.4 0.6 %multiply_bitcast_fusion = f32[3,2]{0,1:T(2,128)} fusion(f32[2,3]{1,0:T(2,128)S(1)} %get-tuple-element.4), kind=kLoop, calls=%fused_computation | loop fusion | flops 6 | bytes 48 | tf_op jit(solution)/shard_map/mul | solution.py:347
